TPU v7x, 32 devices: a whole 2x2x4 slice. The times are simulated.
32 devices in a mesh: grow: 16 (over z, y, x), lat: 2 (over core).
Axes of the slice: x: 2, y: 2, z: 4, core: 2. Of those that a mesh axis runs over, the one named last changes fastest.
Arguments:
- labels: int32 [128, 64, 256], P('grow', 'lat'), may hold values from 0 to 3
- seed_blend: float32 [4, 128, 64, 256], P(None, 'grow', 'lat'), may hold values from 0.02 to 0.6
- potential: float32 [2, 128, 64, 256], P(None, 'grow', 'lat'), may hold values from -3 to 3
- inflow_index: int32 [8, 64, 256], P(None, 'lat'), may hold values from 0 to 15
- liquid_table: float32 [16, 2], replicated, may hold values from -1 to 1
Outputs:
- phase_field: float32 [4, 128, 64, 256], P(None, 'grow', 'lat')
- chem_field: float32 [2, 128, 64, 256], P(None, 'grow', 'lat')
All inputs are finite; a program needn't handle non-finite values.
Results may differ from a plain program's by a relative error of at most 0.0001.
Values sent between devices are 32-bit elements; how exact they have to be, the bound alone decides.
A program may use at most 64 MiB of HBM per device.

v0:
```python
import functools

import jax
import jax.numpy as jnp
from jax import lax
from jax.experimental import pallas as pl
from jax.experimental.pallas import tpu as pltpu
from jax.sharding import PartitionSpec as P

offset_table = ((0.0, 0.0), (0.6, -0.3), (-0.4, 0.5), (-0.2, -0.6))
latent_heat = (0.0, 0.8, 0.8, 0.8)
relax_rate = 0.1
diffusion = 0.05
MESH = pl.DeviceIdType.MESH
ROWS = 8


def advance(phi, chem, lap, temp):
    phi = list(phi) + [1.0 - (phi[0] + phi[1] + phi[2])]
    square = chem[0] * chem[0] + chem[1] * chem[1]
    pull = []
    for a in range(4):
        e0, e1 = offset_table[a]
        p = phi[a]
        w = square - (1.0 - p) * (1.0 - 2.0 * p)
        if a:
            w = w + ((2.0 * e0) * chem[0] + (2.0 * e1) * chem[1] + ((e0 * e0 + e1 * e1) - 2.0 * latent_heat[a] * temp))
        pull.append(p * w)
    mean = 0.25 * ((pull[0] + pull[1]) + (pull[2] + pull[3]))
    new = [phi[a] + relax_rate * ((lap[a] + pull[a]) - mean) for a in range(3)]
    new.append(1.0 - (new[0] + new[1] + new[2]))
    squares = [v * v for v in new]
    growth = [squares[a] - phi[a] * phi[a] for a in range(4)]
    total = (growth[0] + growth[1]) + (growth[2] + growth[3])
    inverse = 1.0 / ((squares[0] + squares[1]) + (squares[2] + squares[3]))
    mobile = diffusion * (0.1 + squares[0])
    out = []
    for k in range(2):
        source = chem[k] * total
        for a in range(1, 4):
            source = source + offset_table[a][k] * growth[a]
        out.append(chem[k] + (mobile * lap[3 + k] - source) * inverse)
    return new, out


def kernel(n, m, labels_h, blend_h, chem_h, index_h, table_h, phase_out, chem_out,
           table, labels, blend, index, own, g, half, from_right, from_left, staged,
           load_sem, send_sem, plane_send, recv_sem, plane_recv, lat_send, lat_recv, out_sem):
    cz, nx, ny = labels.shape
    tiles = nx // ROWS
    me = lax.axis_index("grow")
    lat = lax.axis_index("lat")
    right, left = lax.rem(lat + 1, m), lax.rem(lat + m - 1, m)
    even = lax.rem(me, 2) == 0
    gives, gives_end = me > 0, me > 1
    gets, gets_end = me < n - 1, me < n - 2
    row = lax.broadcasted_iota(jnp.int32, (ROWS, ny), 0)

    loads = [
        pltpu.make_async_copy(labels_h, labels, load_sem.at[0]),
        pltpu.make_async_copy(blend_h, blend, load_sem.at[1]),
        pltpu.make_async_copy(index_h, index, load_sem.at[2]),
        pltpu.make_async_copy(chem_h.at[:, cz - 2 : cz], g.at[3:5, 0:2, 0:nx], load_sem.at[3]),
        pltpu.make_async_copy(table_h, table, load_sem.at[4]),
    ]
    for load in loads:
        load.start()

    barrier = pltpu.get_barrier_semaphore()
    met = jnp.int32(2)
    for step in (-2, -1, 1, 2):
        there = jnp.logical_and(me + step >= 0, me + step < n)
        met = met + there.astype(jnp.int32)

        @pl.when(there)
        def _():
            pl.semaphore_signal(barrier, inc=1, device_id={"grow": me + step}, device_id_type=MESH)

    for side in (left, right):
        pl.semaphore_signal(barrier, inc=1, device_id={"lat": side}, device_id_type=MESH)
    pl.semaphore_wait(barrier, met)

    below, below2 = lax.rem(me + n - 1, n), lax.rem(me + 2 * n - 2, n)
    above = lax.rem(me + 1, n)

    def along(src, dst, send, recv, device):
        return pltpu.make_async_remote_copy(
            src_ref=src, dst_ref=dst, send_sem=send, recv_sem=recv,
            device_id={"grow": device}, device_id_type=MESH)

    end_chem = along(chem_h.at[:, 0:2], g.at[3:5, cz + 2 : cz + 4, 0:nx], send_sem.at[0], recv_sem.at[0], below2)
    end_phi = along(own.at[:, 0:2], g.at[0:3, cz + 2 : cz + 4, 0:nx], send_sem.at[1], recv_sem.at[1], below2)
    head_chem = along(chem_h.at[:, 0:2], g.at[3:5, 2:4, 0:nx], send_sem.at[2], recv_sem.at[2], below)
    head_phi = along(own.at[:, 0:2], g.at[0:3, 2:4, 0:nx], send_sem.at[3], recv_sem.at[3], below)
    body_chem = along(chem_h.at[:, 2:cz], g.at[3:5, 4 : cz + 2, 0:nx], send_sem.at[4], recv_sem.at[4], below)
    pass_chem = along(g.at[3:5, cz + 2 : cz + 4, 0:nx], g.at[3:5, 2:4, 0:nx], send_sem.at[5], recv_sem.at[2], above)
    pass_phi = along(g.at[0:3, cz + 2 : cz + 4, 0:nx], g.at[0:3, 2:4, 0:nx], send_sem.at[6], recv_sem.at[3], above)

    def plane_phi(p):
        return along(own.at[:, pl.ds(p, 1)], g.at[0:3, pl.ds(p + 2, 1), 0:nx], plane_send.at[p], plane_recv.at[p], below)

    odd_gives = jnp.logical_and(gives, jnp.logical_not(even))

    @pl.when(gives_end)
    def _():
        end_chem.start()

    @pl.when(odd_gives)
    def _():
        head_chem.start()

    @pl.when(gives)
    def _():
        body_chem.start()

    loads[0].wait()
    loads[1].wait()

    def initial(p, _):
        kind = labels[p]
        weights = [blend[a, p] for a in range(4)]
        inverse = 1.0 / (1.0 + ((weights[0] + weights[1]) + (weights[2] + weights[3])))
        for a in range(3):
            own[a, p] = (jnp.where(kind == a, 1.0, 0.0) + weights[a]) * inverse
        return _

    lax.fori_loop(0, cz, initial, None)
    for k in range(2):
        for a in range(3):
            g[a, k, 0:nx] = own[a, cz - 2 + k]

    @pl.when(gives_end)
    def _():
        end_phi.start()

    @pl.when(odd_gives)
    def _():
        head_phi.start()

    @pl.when(gives)
    def _():
        def go(p, _):
            plane_phi(p).start()
            return _

        lax.fori_loop(2, cz, go, None)

    loads[2].wait()
    loads[3].wait()
    loads[4].wait()

    def sideways(fields, planes, group):
        return (
            pltpu.make_async_remote_copy(
                src_ref=g.at[fields, planes, nx - ROWS : nx], dst_ref=from_left.at[fields, planes],
                send_sem=lat_send.at[0, group], recv_sem=lat_recv.at[0, group],
                device_id={"lat": right}, device_id_type=MESH),
            pltpu.make_async_remote_copy(
                src_ref=g.at[fields, planes, 0:ROWS], dst_ref=from_right.at[fields, planes],
                send_sem=lat_send.at[1, group], recv_sem=lat_recv.at[1, group],
                device_id={"lat": left}, device_id_type=MESH),
        )

    everything, phases, chemical = slice(0, 5), slice(0, 3), slice(3, 5)
    lat_own = sideways(everything, slice(0, 2), 0)
    lat_head = sideways(everything, slice(2, 4), 1)
    lat_end = sideways(everything, slice(cz + 2, cz + 4), 2)
    lat_chem = sideways(chemical, slice(4, cz + 2), 3)

    def lat_plane(p):
        return sideways(phases, pl.ds(p + 2, 1), 4 + p)

    def start(pair):
        for copy in pair:
            copy.start()

    def wait(pair):
        for copy in pair:
            copy.wait()

    def merge(fields, z):
        for f in fields:
            g[f, z, nx : nx + ROWS] = jnp.where(row < 4, from_right[f, z], from_left[f, z])

    def tile_step(src, z, t):
        def part(f, z, t):
            return src[f, z, t * ROWS : (t + 1) * ROWS]

        after, before = (t + 1) % (tiles + 1), (t + tiles) % (tiles + 1)
        centre, lap = [], []
        for f in range(5):
            c = part(f, z, t)
            up = pltpu.roll(jnp.where(row == 0, part(f, z, after), c), ROWS - 1, 0)
            down = pltpu.roll(jnp.where(row == ROWS - 1, part(f, z, before), c), 1, 0)
            lap.append(
                ((part(f, z + 1, t) + part(f, z - 1, t)) + (up + down))
                + (pltpu.roll(c, ny - 1, 1) + pltpu.roll(c, 1, 1)) - 6.0 * c)
            centre.append(c)
        plane = ((me + 1) * cz - 2 + z).astype(jnp.float32)
        temp = 2.0 * (plane + 0.5) / float(n * cz) - 1.0
        return advance(centre[:3], centre[3:], lap, temp)

    def first(z):
        for t in range(tiles + 1):
            new, chem = tile_step(g, z, t)
            for f, value in enumerate(new[:3] + chem):
                half[f, z, t * ROWS : (t + 1) * ROWS] = value

    def put(o):
        return (
            pltpu.make_async_copy(staged.at[0:4, pl.ds(o, 1)], phase_out.at[:, pl.ds(o, 1)], out_sem.at[0, o]),
            pltpu.make_async_copy(staged.at[4:6, pl.ds(o, 1)], chem_out.at[:, pl.ds(o, 1)], out_sem.at[1, o]),
        )

    def second(z):
        for t in range(tiles):
            new, chem = tile_step(half, z, t)
            for f, value in enumerate(new + chem):
                staged[f, z - 2, t * ROWS : (t + 1) * ROWS] = value
        start(put(z - 2))

    def firsts(low, high):
        lax.fori_loop(low, high, lambda z, _: first(z), None)

    def seconds(low, high):
        lax.fori_loop(low, high, lambda z, _: second(z), None)

    @pl.when(gets)
    def _():
        start(lat_own)

        @pl.when(jnp.logical_and(even, gets_end))
        def _():
            end_chem.wait_recv()
            pass_chem.start()
            end_phi.wait_recv()
            pass_phi.start()
            start(lat_end)

        @pl.when(even)
        def _():
            head_chem.wait_recv()
            head_phi.wait_recv()
            start(lat_head)

        body_chem.wait_recv()
        start(lat_chem)
        wait(lat_own)
        for z in (0, 1):
            merge(range(5), z)

        @pl.when(even)
        def _():
            wait(lat_head)
            for z in (2, 3):
                merge(range(5), z)
            firsts(1, 3)

        wait(lat_chem)
        lax.fori_loop(4, cz + 2, lambda z, _: merge((3, 4), z), None)

        def plane(p, _):
            z = p + 2
            plane_phi(p).wait_recv()
            start(lat_plane(p))
            wait(lat_plane(p))
            merge(range(3), z)

            @pl.when(jnp.logical_or(even, p >= 4))
            def _():
                first(z - 1)

            @pl.when(jnp.logical_or(even, p >= 6))
            def _():
                second(z - 2)

        lax.fori_loop(2, cz, plane, None)

        @pl.when(jnp.logical_not(even))
        def _():
            head_chem.wait_recv()
            head_phi.wait_recv()
            start(lat_head)

            @pl.when(gets_end)
            def _():
                end_chem.wait_recv()
                end_phi.wait_recv()
                start(lat_end)

            wait(lat_head)
            for z in (2, 3):
                merge(range(5), z)
            firsts(1, 5)
            seconds(2, 6)

        @pl.when(gets_end)
        def _():
            wait(lat_end)
            for z in (cz + 2, cz + 3):
                merge(range(5), z)
            firsts(cz + 1, cz + 3)

        @pl.when(jnp.logical_not(gets_end))
        def _():
            for f in range(5):
                g[f, cz + 2] = g[f, cz + 1]
            first(cz + 1)
            for f in range(5):
                half[f, cz + 2] = half[f, cz + 1]

        seconds(cz, cz + 2)

    @pl.when(jnp.logical_not(gets))
    def _():
        def entering(o, _):
            kind = index[o]
            for a in range(4):
                staged[a, o] = jnp.full((nx, ny), 1.0 if a == 0 else 0.0, jnp.float32)
            for k in range(2):
                value = jnp.zeros((nx, ny), jnp.float32)
                for liquid in range(table.shape[1]):
                    value = jnp.where(kind == liquid, table[k, liquid], value)
                staged[4 + k, o] = value
            start(put(o))
            return _

        lax.fori_loop(0, cz, entering, None)

    @pl.when(gives_end)
    def _():
        end_chem.wait_send()
        end_phi.wait_send()

    @pl.when(odd_gives)
    def _():
        head_chem.wait_send()
        head_phi.wait_send()

    @pl.when(gives)
    def _():
        body_chem.wait_send()

        def gone(p, _):
            plane_phi(p).wait_send()
            return _

        lax.fori_loop(2, cz, gone, None)

    @pl.when(jnp.logical_and(even, gets_end))
    def _():
        pass_chem.wait_send()
        pass_phi.wait_send()

    def written(o, _):
        wait(put(o))
        return _

    lax.fori_loop(0, cz, written, None)


def body(labels, seed_blend, potential, inflow_index, liquid_table):
    n, m = lax.axis_size("grow"), lax.axis_size("lat")
    cz, nx, ny = labels.shape
    anywhere = pl.BlockSpec(memory_space=pl.ANY)
    dma = pltpu.SemaphoreType.DMA
    f32 = jnp.float32
    return pl.pallas_call(
        functools.partial(kernel, n, m),
        out_shape=(jax.ShapeDtypeStruct((4, cz, nx, ny), f32), jax.ShapeDtypeStruct((2, cz, nx, ny), f32)),
        in_specs=[pl.BlockSpec(memory_space=pltpu.HBM)] * 5,
        out_specs=(anywhere, anywhere),
        scratch_shapes=[
            pltpu.SMEM(liquid_table.shape[::-1], f32),
            pltpu.VMEM((cz, nx, ny), jnp.int32),
            pltpu.VMEM((4, cz, nx, ny), f32),
            pltpu.VMEM((cz, nx, ny), jnp.int32),
            pltpu.VMEM((3, cz, nx, ny), f32),
            pltpu.VMEM((5, cz + 4, nx + ROWS, ny), f32),
            pltpu.VMEM((5, cz + 4, nx + ROWS, ny), f32),
            pltpu.VMEM((5, cz + 4, ROWS, ny), f32),
            pltpu.VMEM((5, cz + 4, ROWS, ny), f32),
            pltpu.VMEM((6, cz, nx, ny), f32),
            dma((5,)),
            dma((7,)),
            dma((cz,)),
            dma((5,)),
            dma((cz,)),
            dma((2, 4 + cz)),
            dma((2, 4 + cz)),
            dma((2, cz)),
        ],
        compiler_params=pltpu.CompilerParams(collective_id=0, has_side_effects=True, vmem_limit_bytes=12 << 20),
    )(labels, seed_blend, potential, inflow_index, liquid_table.T)


def solution(mesh):
    in_specs = (
        P("grow", "lat", None),
        P(None, "grow", "lat", None),
        P(None, "grow", "lat", None),
        P(None, "lat", None),
        P(),
    )
    out_specs = (P(None, "grow", "lat", None), P(None, "grow", "lat", None))
    return jax.shard_map(body, mesh=mesh, in_specs=in_specs, out_specs=out_specs, check_vma=False)
```

profile of v0, /device:TPU:7, one launch (start us, length us, event | category | flops | bytes accessed | tf_op | source)
XLA Modules:
  0.0 50.9 jit_solution(1876523189259968911)
XLA Ops:
  0.6 0.0 copy-start.4
  0.6 0.7 %copy-done.4 = f32[16,2]{0,1:T(2,128)S(1)} copy-done((f32[16,2]{0,1:T(2,128)S(1)}, f32[16,2]{0,1:T(2,128)}, u32[]{:S(2)}) %copy-start.4) | copy-done | bytes 152
  1.3 0.0 copy-start
  1.3 1.2 %copy-done = f32[4,8,32,256]{3,2,1,0:T(8,128)S(1)} copy-done((f32[4,8,32,256]{3,2,1,0:T(8,128)S(1)}, f32[4,8,32,256]{3,2,1,0:T(8,128)}, u32[]{:S(2)}) %copy-start) | copy-done | bytes 1048600
  2.5 0.0 copy-start.1
  2.5 1.0 %copy-done.1 = f32[2,8,32,256]{3,2,1,0:T(8,128)S(1)} copy-done((f32[2,8,32,256]{3,2,1,0:T(8,128)S(1)}, f32[2,8,32,256]{3,2,1,0:T(8,128)}, u32[]{:S(2)}) %copy-start.1) | copy-done | bytes 524312
  3.6 0.0 copy-start.2
  3.6 0.9 %copy-done.2 = s32[8,32,256]{2,1,0:T(8,128)S(1)} copy-done((s32[8,32,256]{2,1,0:T(8,128)S(1)}, s32[8,32,256]{2,1,0:T(8,128)}, u32[]{:S(2)}) %copy-start.2) | copy-done | bytes 262168
  4.5 0.0 copy-start.3
  4.5 0.9 %copy-done.3 = s32[8,32,256]{2,1,0:T(8,128)S(1)} copy-done((s32[8,32,256]{2,1,0:T(8,128)S(1)}, s32[8,32,256]{2,1,0:T(8,128)}, u32[]{:S(2)}) %copy-start.3) | copy-done | bytes 262168
  5.5 43.6 %shard_map.68 = (f32[4,8,32,256]{3,2,1,0:T(8,128)S(1)}, f32[2,8,32,256]{3,2,1,0:T(8,128)S(1)}) custom-call(s32[8,32,256]{2,1,0:T(8,128)S(1)} %copy-done.2, f32[4,8,32,256]{3,2,1,0:T(8,128)S(1)} %copy-done, f32[2,8,32,256]{3,2,1,0:T(8,128)S(1)} %copy-done.1, s32[8,32,256]{2,1,0:T(8,128)S(1)} %copy-done.3, f32[2,16]{1,0:T(2,128)S(1)} %bitcast.1), custom_call_target="tpu_custom_call" | custom-call | tf_op jit(solution)/shard_map/pallas_call | solution.py:368
  49.1 1.0 %copy.9 = f32[4,8,32,256]{3,2,1,0:T(8,128)} copy(f32[4,8,32,256]{3,2,1,0:T(8,128)S(1)} %get-tuple-element.4) | data formatting | bytes 2097152
  50.1 0.8 %copy.10 = f32[2,8,32,256]{3,2,1,0:T(8,128)} copy(f32[2,8,32,256]{3,2,1,0:T(8,128)S(1)} %get-tuple-element.5) | data formatting | bytes 1048576
Async XLA Ops:
  0.6 0.7 %copy-start.4 = (f32[16,2]{0,1:T(2,128)S(1)}, f32[16,2]{0,1:T(2,128)}, u32[]{:S(2)}) copy-start(f32[16,2]{0,1:T(2,128)} %param.9) | copy-start | bytes 388
  1.3 1.2 %copy-start = (f32[4,8,32,256]{3,2,1,0:T(8,128)S(1)}, f32[4,8,32,256]{3,2,1,0:T(8,128)}, u32[]{:S(2)}) copy-start(f32[4,8,32,256]{3,2,1,0:T(8,128)} %blend_h.1) | copy-start | bytes 3145732
  2.5 1.0 %copy-start.1 = (f32[2,8,32,256]{3,2,1,0:T(8,128)S(1)}, f32[2,8,32,256]{3,2,1,0:T(8,128)}, u32[]{:S(2)}) copy-start(f32[2,8,32,256]{3,2,1,0:T(8,128)} %chem_h.1) | copy-start | bytes 1572868
  3.6 0.9 %copy-start.2 = (s32[8,32,256]{2,1,0:T(8,128)S(1)}, s32[8,32,256]{2,1,0:T(8,128)}, u32[]{:S(2)}) copy-start(s32[8,32,256]{2,1,0:T(8,128)} %labels_h.1) | copy-start | bytes 786436
  4.5 0.9 %copy-start.3 = (s32[8,32,256]{2,1,0:T(8,128)S(1)}, s32[8,32,256]{2,1,0:T(8,128)}, u32[]{:S(2)}) copy-start(s32[8,32,256]{2,1,0:T(8,128)} %index_h.1) | copy-start | bytes 786436
where the time goes:
time: 51.2 us; the launch traced here: 50.9 us
  Pallas kernels  43.6 us (85%)
  local copies, waits for them, and re-layouts  6.6 us (13%)
  between operations  0.65 us (1%)
    pallas_call x1, Pallas kernels, body(): pl.pallas_call(functools.partial(kernel, n, m), out_shape=(jax.ShapeDtype...  43.6 us
    unnamed x12, local copies, waits for them, and re-layouts  6.6 us

commit v1 on v0

--- a/solution.py
+++ b/solution.py
@@ -391,7 +391,7 @@
             dma((2, cz)),
         ],
         compiler_params=pltpu.CompilerParams(collective_id=0, has_side_effects=True, vmem_limit_bytes=12 << 20),
-    )(labels, seed_blend, potential, inflow_index, liquid_table.T)
+    )(*(pltpu.with_memory_space_constraint(a, pltpu.HBM) for a in (labels, seed_blend, potential, inflow_index, liquid_table.T)))
 
 
 def solution(mesh):

time: 51.2 us -> 46.2 us (0.902)
  local copies, waits for them, and re-layouts: 6.6 us -> 1.77 us
    unnamed x12 -> x2, local copies, waits for them, and re-layouts: 6.6 us -> 1.77 us
where the time goes in v1:
time: 46.2 us; the launch traced here: 46.1 us
  Pallas kernels  43.7 us (95%)
  local copies, waits for them, and re-layouts  1.77 us (4%)
  between operations  0.64 us (1%)
    pallas_call x1, Pallas kernels, body(): pl.pallas_call(functools.partial(kernel, n, m), out_shape=(jax.ShapeDtype...  43.7 us
    unnamed x2, local copies, waits for them, and re-layouts  1.77 us

profile of v1, /device:TPU:7, one launch (start us, length us, event | category | flops | bytes accessed | tf_op | source)
XLA Modules:
  0.0 46.1 jit_solution(5719199616373608798)
XLA Ops:
  0.6 43.7 %shard_map.68 = (f32[4,8,32,256]{3,2,1,0:T(8,128)S(1)}, f32[2,8,32,256]{3,2,1,0:T(8,128)S(1)}) custom-call(s32[8,32,256]{2,1,0:T(8,128)} %labels_h.1, f32[4,8,32,256]{3,2,1,0:T(8,128)} %blend_h.1, f32[2,8,32,256]{3,2,1,0:T(8,128)} %chem_h.1, s32[8,32,256]{2,1,0:T(8,128)} %index_h.1, f32[2,16]{1,0:T(2,128)} %bitcast.1), custom_call_target="tpu_custom_call" | custom-call | tf_op jit(solution)/shard_map/pallas_call | solution.py:368
  44.3 1.0 %copy.9 = f32[4,8,32,256]{3,2,1,0:T(8,128)} copy(f32[4,8,32,256]{3,2,1,0:T(8,128)S(1)} %get-tuple-element.4) | data formatting | bytes 2097152
  45.3 0.8 %copy.10 = f32[2,8,32,256]{3,2,1,0:T(8,128)} copy(f32[2,8,32,256]{3,2,1,0:T(8,128)S(1)} %get-tuple-element.5) | data formatting | bytes 1048576

commit v2 on v1

--- a/solution.py
+++ b/solution.py
@@ -43,16 +43,18 @@
     return new, out
 
 
-def kernel(n, m, labels_h, blend_h, chem_h, index_h, table_h, phase_out, chem_out,
-           table, labels, blend, index, own, g, half, from_right, from_left, staged,
-           load_sem, send_sem, plane_send, recv_sem, plane_recv, lat_send, lat_recv, out_sem):
+def kernel(n, m, labels_h, blend_h, chem_h, index_h, table_h, staged,
+           table, labels, blend, index, own, g, half, from_right, from_left, relay,
+           load_sem, send_sem, plane_send, recv_sem, plane_recv, lat_send, lat_recv):
     cz, nx, ny = labels.shape
     tiles = nx // ROWS
     me = lax.axis_index("grow")
     lat = lax.axis_index("lat")
     right, left = lax.rem(lat + 1, m), lax.rem(lat + m - 1, m)
     even = lax.rem(me, 2) == 0
-    gives, gives_end = me > 0, me > 1
+    corner = lax.rem(me, 4)
+    gives, gives_end = me > 0, jnp.logical_and(me > 1, corner != 0)
+    gives_via, gets_via = jnp.logical_and(me > 1, corner == 0), jnp.logical_and(me > 4, corner == 2)
     gets, gets_end = me < n - 1, me < n - 2
     row = lax.broadcasted_iota(jnp.int32, (ROWS, ny), 0)
 
@@ -76,12 +78,20 @@
         def _():
             pl.semaphore_signal(barrier, inc=1, device_id={"grow": me + step}, device_id_type=MESH)
 
+    for step in (-4, 4):
+        there = jnp.logical_and(corner == 2, jnp.logical_and(me + step > 0, me + step < n))
+        met = met + there.astype(jnp.int32)
+
+        @pl.when(there)
+        def _():
+            pl.semaphore_signal(barrier, inc=1, device_id={"grow": me + step}, device_id_type=MESH)
+
     for side in (left, right):
         pl.semaphore_signal(barrier, inc=1, device_id={"lat": side}, device_id_type=MESH)
     pl.semaphore_wait(barrier, met)
 
     below, below2 = lax.rem(me + n - 1, n), lax.rem(me + 2 * n - 2, n)
-    above = lax.rem(me + 1, n)
+    above, above2, below4 = lax.rem(me + 1, n), lax.rem(me + 2, n), lax.rem(me + n - 4, n)
 
     def along(src, dst, send, recv, device):
         return pltpu.make_async_remote_copy(
@@ -96,6 +106,11 @@
     pass_chem = along(g.at[3:5, cz + 2 : cz + 4, 0:nx], g.at[3:5, 2:4, 0:nx], send_sem.at[5], recv_sem.at[2], above)
     pass_phi = along(g.at[0:3, cz + 2 : cz + 4, 0:nx], g.at[0:3, 2:4, 0:nx], send_sem.at[6], recv_sem.at[3], above)
 
+    via_chem = along(chem_h.at[:, 0:2], relay.at[3:5], send_sem.at[0], recv_sem.at[5], above2)
+    via_phi = along(own.at[:, 0:2], relay.at[0:3], send_sem.at[1], recv_sem.at[6], above2)
+    far_chem = along(relay.at[3:5], g.at[3:5, cz + 2 : cz + 4, 0:nx], send_sem.at[7], recv_sem.at[0], below4)
+    far_phi = along(relay.at[0:3], g.at[0:3, cz + 2 : cz + 4, 0:nx], send_sem.at[8], recv_sem.at[1], below4)
+
     def plane_phi(p):
         return along(own.at[:, pl.ds(p, 1)], g.at[0:3, pl.ds(p + 2, 1), 0:nx], plane_send.at[p], plane_recv.at[p], below)
 
@@ -104,6 +119,10 @@
     @pl.when(gives_end)
     def _():
         end_chem.start()
+
+    @pl.when(gives_via)
+    def _():
+        via_chem.start()
 
     @pl.when(odd_gives)
     def _():
@@ -133,6 +152,10 @@
     def _():
         end_phi.start()
 
+    @pl.when(gives_via)
+    def _():
+        via_phi.start()
+
     @pl.when(odd_gives)
     def _():
         head_phi.start()
@@ -148,6 +171,13 @@
     loads[2].wait()
     loads[3].wait()
     loads[4].wait()
+
+    @pl.when(gets_via)
+    def _():
+        via_chem.wait_recv()
+        far_chem.start()
+        via_phi.wait_recv()
+        far_phi.start()
 
     def sideways(fields, planes, group):
         return (
@@ -206,18 +236,11 @@
             for f, value in enumerate(new[:3] + chem):
                 half[f, z, t * ROWS : (t + 1) * ROWS] = value
 
-    def put(o):
-        return (
-            pltpu.make_async_copy(staged.at[0:4, pl.ds(o, 1)], phase_out.at[:, pl.ds(o, 1)], out_sem.at[0, o]),
-            pltpu.make_async_copy(staged.at[4:6, pl.ds(o, 1)], chem_out.at[:, pl.ds(o, 1)], out_sem.at[1, o]),
-        )
-
     def second(z):
         for t in range(tiles):
             new, chem = tile_step(half, z, t)
             for f, value in enumerate(new + chem):
                 staged[f, z - 2, t * ROWS : (t + 1) * ROWS] = value
-        start(put(z - 2))
 
     def firsts(low, high):
         lax.fori_loop(low, high, lambda z, _: first(z), None)
@@ -322,7 +345,6 @@
                 for liquid in range(table.shape[1]):
                     value = jnp.where(kind == liquid, table[k, liquid], value)
                 staged[4 + k, o] = value
-            start(put(o))
             return _
 
         lax.fori_loop(0, cz, entering, None)
@@ -331,6 +353,16 @@
     def _():
         end_chem.wait_send()
         end_phi.wait_send()
+
+    @pl.when(gives_via)
+    def _():
+        via_chem.wait_send()
+        via_phi.wait_send()
+
+    @pl.when(gets_via)
+    def _():
+        far_chem.wait_send()
+        far_phi.wait_send()
 
     @pl.when(odd_gives)
     def _():
@@ -352,24 +384,29 @@
         pass_chem.wait_send()
         pass_phi.wait_send()
 
-    def written(o, _):
-        wait(put(o))
-        return _
-
-    lax.fori_loop(0, cz, written, None)
+
+def flush(staged, phase_out, chem_out, sem):
+    copies = (
+        pltpu.make_async_copy(staged.at[0:4], phase_out, sem.at[0]),
+        pltpu.make_async_copy(staged.at[4:6], chem_out, sem.at[1]),
+    )
+    for copy in copies:
+        copy.start()
+    for copy in copies:
+        copy.wait()
 
 
 def body(labels, seed_blend, potential, inflow_index, liquid_table):
     n, m = lax.axis_size("grow"), lax.axis_size("lat")
     cz, nx, ny = labels.shape
-    anywhere = pl.BlockSpec(memory_space=pl.ANY)
     dma = pltpu.SemaphoreType.DMA
     f32 = jnp.float32
-    return pl.pallas_call(
+    vmem, hbm = pl.BlockSpec(memory_space=pltpu.VMEM), pl.BlockSpec(memory_space=pltpu.HBM)
+    staged = pl.pallas_call(
         functools.partial(kernel, n, m),
-        out_shape=(jax.ShapeDtypeStruct((4, cz, nx, ny), f32), jax.ShapeDtypeStruct((2, cz, nx, ny), f32)),
-        in_specs=[pl.BlockSpec(memory_space=pltpu.HBM)] * 5,
-        out_specs=(anywhere, anywhere),
+        out_shape=pltpu.VMEM((6, cz, nx, ny), f32),
+        in_specs=[hbm] * 5,
+        out_specs=vmem,
         scratch_shapes=[
             pltpu.SMEM(liquid_table.shape[::-1], f32),
             pltpu.VMEM((cz, nx, ny), jnp.int32),
@@ -380,18 +417,25 @@
             pltpu.VMEM((5, cz + 4, nx + ROWS, ny), f32),
             pltpu.VMEM((5, cz + 4, ROWS, ny), f32),
             pltpu.VMEM((5, cz + 4, ROWS, ny), f32),
-            pltpu.VMEM((6, cz, nx, ny), f32),
+            pltpu.VMEM((5, 2, nx, ny), f32),
             dma((5,)),
+            dma((9,)),
+            dma((cz,)),
             dma((7,)),
-            dma((cz,)),
-            dma((5,)),
             dma((cz,)),
             dma((2, 4 + cz)),
             dma((2, 4 + cz)),
-            dma((2, cz)),
         ],
         compiler_params=pltpu.CompilerParams(collective_id=0, has_side_effects=True, vmem_limit_bytes=12 << 20),
     )(*(pltpu.with_memory_space_constraint(a, pltpu.HBM) for a in (labels, seed_blend, potential, inflow_index, liquid_table.T)))
+    return pl.pallas_call(
+        flush,
+        out_shape=(jax.ShapeDtypeStruct((4, cz, nx, ny), f32), jax.ShapeDtypeStruct((2, cz, nx, ny), f32)),
+        in_specs=[pl.BlockSpec(memory_space=pl.ANY)],
+        out_specs=(hbm, hbm),
+        scratch_shapes=[dma((2,))],
+        compiler_params=pltpu.CompilerParams(vmem_limit_bytes=1 << 20),
+    )(pltpu.with_memory_space_constraint(staged, pltpu.VMEM))
 
 
 def solution(mesh):

time: 46.2 us -> 40.6 us (0.88)
  Pallas kernels: 43.7 us -> 39.8 us
  local copies, waits for them, and re-layouts: 1.77 us -> 0 us
    pallas_call x1 -> x2, Pallas kernels: 43.7 us -> 39.8 us  [the longest x1 38.7 us: body(): pl.pallas_call(functools.partial(kernel, n, m), out_shape=pltpu.VMEM((6,...]
    unnamed x2 -> x0, local copies, waits for them, and re-layouts: 1.77 us -> none
where the time goes in v2:
time: 40.6 us; the launch traced here: 40.5 us
  Pallas kernels  39.8 us (98%)
  between operations  0.64 us (2%)
    pallas_call x1, Pallas kernels, body(): pl.pallas_call(functools.partial(kernel, n, m), out_shape=pltpu.VMEM((6,...  38.7 us
    pallas_call x1, Pallas kernels, body(): pl.pallas_call(flush, out_shape=(jax.ShapeDtypeStruct((4, cz, nx, ny), f3...  1.16 us

profile of v2, /device:TPU:7, one launch (start us, length us, event | category | flops | bytes accessed | tf_op | source)
XLA Modules:
  0.0 40.5 jit_solution(17229876511390743375)
XLA Ops:
  0.6 38.7 %shard_map.68.staged = f32[6,8,32,256]{3,2,1,0:T(8,128)S(1)} custom-call(s32[8,32,256]{2,1,0:T(8,128)} %labels_h.1, f32[4,8,32,256]{3,2,1,0:T(8,128)} %blend_h.1, f32[2,8,32,256]{3,2,1,0:T(8,128)} %chem_h.1, s32[8,32,256]{2,1,0:T(8,128)} %index_h.1, f32[2,16]{1,0:T(2,128)} %bitcast.1), custom_call_target="tpu_custom_call" | custom-call | tf_op jit(solution)/shard_map/pallas_call | solution.py:405
  39.3 1.2 %shard_map.69 = (f32[4,8,32,256]{3,2,1,0:T(8,128)}, f32[2,8,32,256]{3,2,1,0:T(8,128)}) custom-call(f32[6,8,32,256]{3,2,1,0:T(8,128)S(1)} %shard_map.68.staged), custom_call_target="tpu_custom_call" | custom-call | tf_op jit(solution)/shard_map/pallas_call | solution.py:431

commit v3 on v2

v3 whole, which is shorter than its diff:
```python
import functools

import jax
import jax.numpy as jnp
from jax import lax
from jax.experimental import pallas as pl
from jax.experimental.pallas import tpu as pltpu
from jax.sharding import PartitionSpec as P

offset_table = ((0.0, 0.0), (0.6, -0.3), (-0.4, 0.5), (-0.2, -0.6))
latent_heat = (0.0, 0.8, 0.8, 0.8)
relax_rate = 0.1
diffusion = 0.05
MESH = pl.DeviceIdType.MESH
ROWS = 8


def advance(phi, chem, lap, temp):
    phi = list(phi) + [1.0 - (phi[0] + phi[1] + phi[2])]
    square = chem[0] * chem[0] + chem[1] * chem[1]
    pull = []
    for a in range(4):
        e0, e1 = offset_table[a]
        p = phi[a]
        w = square - (1.0 - p) * (1.0 - 2.0 * p)
        if a:
            w = w + ((2.0 * e0) * chem[0] + (2.0 * e1) * chem[1] + ((e0 * e0 + e1 * e1) - 2.0 * latent_heat[a] * temp))
        pull.append(p * w)
    mean = 0.25 * ((pull[0] + pull[1]) + (pull[2] + pull[3]))
    new = [phi[a] + relax_rate * ((lap[a] + pull[a]) - mean) for a in range(3)]
    new.append(1.0 - (new[0] + new[1] + new[2]))
    squares = [v * v for v in new]
    growth = [squares[a] - phi[a] * phi[a] for a in range(4)]
    total = (growth[0] + growth[1]) + (growth[2] + growth[3])
    inverse = 1.0 / ((squares[0] + squares[1]) + (squares[2] + squares[3]))
    mobile = diffusion * (0.1 + squares[0])
    out = []
    for k in range(2):
        source = chem[k] * total
        for a in range(1, 4):
            source = source + offset_table[a][k] * growth[a]
        out.append(chem[k] + (mobile * lap[3 + k] - source) * inverse)
    return new, out


BASE = 32
PLANE, EDGES, MID, LAST, HEAD, PASS_MID, PASS_LAST, END, END_NEXT = range(1, 10)


def schedule(kind, cz):
    pair, head, top = cz - 2, cz - 1, cz + 2
    none = (0, 0)

    def step(event, sent=None, landed=None, halo=none, own=none, two=none):
        return (event, 0 if sent is None else sent + 1, 0 if landed is None else landed + 1, halo, own, two)

    if kind == 0:
        return [
            step(PLANE, 0, cz),
            step(PLANE, 1, 0, none, (1, 1)),
            step(PLANE, 2, 1, (2, 1), (2, 1)),
            *(step(PLANE, p, p - 1, (p, 1), (p, 1), (p - 1, 1)) for p in range(3, pair)),
            step(EDGES, pair, pair - 1, (pair, 1), (pair, 1), (pair - 1, 1)),
            step(0, None, pair, (pair + 1, 3)),
            step(MID, None, None, none, (pair + 1, 1), (pair, 1)),
            step(LAST, None, None, none, (cz, 3), (cz - 1, 3)),
        ]
    body = [step(PLANE, 2), step(PLANE, 3, 2)]
    if kind == 1:
        return [
            *body,
            step(PLANE, 4, 3),
            step(PLANE, 5, 4, (5, 1), (5, 1)),
            *(step(PLANE, p, p - 1, (p, 1), (p, 1), (p - 1, 1) if p > 6 else none) for p in range(6, pair)),
            step(EDGES, pair, pair - 1, (pair, 1), (pair, 1), (pair - 1, 1) if pair > 6 else none),
            step(0, None, pair, (pair + 1, 2)),
            step(MID, None, None, none, (pair + 1, 1), (pair, 1)),
            step(LAST, None, None, none, (cz, 1), (cz - 1, 1)),
            step(HEAD, head),
            step(0, None, head, (2, 3)),
            step(PASS_MID, None, None, none, (4, 1), (5, 1)),
            step(PASS_LAST, None, None, none, (1, 3), (2, 3)),
            step(END, cz),
            step(0, None, cz, (cz + 1, 1), (cz + 1, 1), (cz, 1)),
            step(END_NEXT, None, None, none, (top, 1), (cz + 1, 1)),
        ]
    return [
        *body,
        step(END, cz, 3),
        step(PLANE, 4, cz),
        step(END_NEXT, None, 4, (5, 1), (5, 1)),
        step(PLANE, 5),
        *(step(PLANE, p, p - 1, (p, 1), (p, 1), (p - 1, 1) if p > 6 else none) for p in range(6, pair)),
        step(HEAD, head, pair - 1, (pair, 1), (pair, 1), (pair - 1, 1) if pair > 6 else none),
        step(EDGES, pair, head, (2, 3)),
        step(PASS_MID, None, None, none, (4, 1), (5, 1)),
        step(PASS_LAST, None, None, none, (1, 3), (2, 3)),
        step(MID, None, pair, (pair + 1, 3), (pair + 1, 1), (pair, 1)),
        step(LAST, None, None, none, (cz, 3), (cz - 1, 3)),
    ]


def pack(step):
    event, sent, landed, halo, own, two = step
    work = 0
    for low, number in (two, own, halo):
        work = work * (4 * BASE) + low + BASE * number
    return event + BASE * (sent + BASE * landed), work


def kernel(n, m, labels_h, blend_h, chem_h, index_h, table_h, staged,
           table, labels, blend, index, own, g, half, from_right, from_left, relay,
           load_sem, send_sem, recv_sem, plane_send, plane_recv, lat_send, lat_recv, go):
    cz, nx, ny = labels.shape
    tiles = nx // ROWS
    inner = tuple(range(tiles))
    top = cz + 2
    me = lax.axis_index("grow")
    lat = lax.axis_index("lat")
    right, left = lax.rem(lat + 1, m), lax.rem(lat + m - 1, m)
    corner = lax.rem(me, 4)
    even = lax.rem(me, 2) == 0
    odd = jnp.logical_not(even)
    gives, gets = me > 0, me < n - 1
    gets_end = me < n - 2
    gives_via = jnp.logical_and(corner == 0, me > 0)
    gets_via = jnp.logical_and(corner == 2, me > 4)
    row = lax.broadcasted_iota(jnp.int32, (ROWS, ny), 0)

    barrier = pltpu.get_barrier_semaphore()

    def greet(there, device):
        @pl.when(there)
        def _():
            pl.semaphore_signal(barrier, inc=1, device_id={"grow": device}, device_id_type=MESH)

    greet(odd, me - 1)
    greet(even, me + 1)
    greet(jnp.logical_and(odd, me + 1 < n), me + 1)
    greet(corner == 0, me + 2)
    greet(gets_via, me - 2)
    greet(jnp.logical_and(corner == 2, me + 4 < n), me + 4)
    for side in (left, right):
        pl.semaphore_signal(barrier, inc=1, device_id={"lat": side}, device_id_type=MESH)

    loads = [
        pltpu.make_async_copy(labels_h, labels, load_sem.at[0]),
        pltpu.make_async_copy(blend_h, blend, load_sem.at[1]),
        pltpu.make_async_copy(index_h, index, load_sem.at[2]),
        pltpu.make_async_copy(chem_h.at[:, cz - 2 : cz], g.at[3:5, 0:2, 0:nx], load_sem.at[3]),
        pltpu.make_async_copy(table_h, table, load_sem.at[4]),
    ]
    for load in loads:
        load.start()

    met = 3 + jnp.where(even, (me > 0).astype(jnp.int32) + (corner == 2).astype(jnp.int32)
                        + gets_via.astype(jnp.int32) + gives_via.astype(jnp.int32), 0)
    pl.semaphore_wait(barrier, met)

    @pl.when(even)
    def _():
        pl.semaphore_signal(go, inc=1, device_id={"grow": me + 1}, device_id_type=MESH)

    def to(step):
        return lax.rem(me + n + step, n)

    def along(src, dst, send, recv, device):
        return pltpu.make_async_remote_copy(
            src_ref=src, dst_ref=dst, send_sem=send_sem.at[send], recv_sem=recv_sem.at[recv],
            device_id={"grow": device}, device_id_type=MESH)

    low, middle, high = pl.ds(0, ROWS), pl.ds(ROWS, nx - 2 * ROWS), pl.ds(nx - ROWS, ROWS)
    rows = pl.ds(0, nx)

    end = (
        along(chem_h.at[:, 0:2], g.at[3:5, top : top + 2, rows], 0, 0, to(-2)),
        along(own.at[:, 0:1], g.at[0:3, top : top + 1, rows], 1, 1, to(-2)),
        along(own.at[:, 1:2], g.at[0:3, top + 1 : top + 2, rows], 2, 2, to(-2)),
    )
    via = (
        along(chem_h.at[:, 0:2], relay.at[3:5], 0, 13, to(2)),
        along(own.at[:, 0:1], relay.at[0:3, 0:1], 1, 14, to(2)),
        along(own.at[:, 1:2], relay.at[0:3, 1:2], 2, 15, to(2)),
    )
    far = (
        along(relay.at[3:5], g.at[3:5, top : top + 2, rows], 13, 0, to(-4)),
        along(relay.at[0:3, 0:1], g.at[0:3, top : top + 1, rows], 14, 1, to(-4)),
        along(relay.at[0:3, 1:2], g.at[0:3, top + 1 : top + 2, rows], 15, 2, to(-4)),
    )
    head_chem = along(chem_h.at[:, 0:2], g.at[3:5, 2:4, rows], 3, 3, to(-1))
    lead_chem = along(chem_h.at[:, 2:4], g.at[3:5, 4:6, rows], 16, 16, to(-1))
    body_chem = along(chem_h.at[:, 4:cz], g.at[3:5, 6:top, rows], 4, 4, to(-1))
    def banded(src, dst, send, recv, device):
        return [
            along(src(planes, band), dst(planes, band), send + k, recv + k, device)
            for k, (planes, band) in enumerate(
                ((pl.ds(0, 2), low), (pl.ds(0, 2), high), (pl.ds(0, 1), middle), (pl.ds(1, 1), middle)))
        ]

    final_own, final_g = own.at[:, cz - 2 : cz], g.at[0:3, cz:top]
    last_phi = banded(lambda p, r: final_own.at[:, p, r], lambda p, r: final_g.at[:, p, r], 5, 5, to(-1))
    end_g, head_g = g.at[0:3, top : top + 2], g.at[0:3, 2:4]
    pass_chem = along(g.at[3:5, top : top + 2, rows], g.at[3:5, 2:4, rows], 17, 3, to(1))
    pass_phi = banded(lambda p, r: end_g.at[:, p, r], lambda p, r: head_g.at[:, p, r], 9, 9, to(1))
    pass_phi = [pass_phi[0], pass_phi[1], pass_phi[3], pass_phi[2]]

    def plane_phi(p):
        return pltpu.make_async_remote_copy(
            src_ref=own.at[:, pl.ds(p, 1)], dst_ref=g.at[0:3, pl.ds(p + 2, 1), rows],
            send_sem=plane_send.at[p], recv_sem=plane_recv.at[p],
            device_id={"grow": to(-1)}, device_id_type=MESH)

    gives_end = jnp.logical_and(me > 1, corner != 0)
    even_end = jnp.logical_and(corner == 2, me > 1)
    odd_end = jnp.logical_and(odd, me > 1)

    @pl.when(odd)
    def _():
        head_chem.start()

    @pl.when(gives)
    def _():
        lead_chem.start()
        body_chem.start()

    @pl.when(even_end)
    def _():
        end[0].start()

    @pl.when(gives_via)
    def _():
        via[0].start()

    loads[0].wait()
    loads[1].wait()

    def initial(p, _):
        kind = labels[p]
        weights = [blend[a, p] for a in range(4)]
        inverse = 1.0 / (1.0 + ((weights[0] + weights[1]) + (weights[2] + weights[3])))
        for a in range(3):
            own[a, p] = (jnp.where(kind == a, 1.0, 0.0) + weights[a]) * inverse
        return _

    lax.fori_loop(0, cz, initial, None)

    @pl.when(odd)
    def _():
        plane_phi(0).start()
        plane_phi(1).start()

    @pl.when(even_end)
    def _():
        end[1].start()
        end[2].start()

    @pl.when(gives_via)
    def _():
        via[1].start()
        via[2].start()

    def planes(low_p, high_p, act):
        def step(p, _):
            act(plane_phi(p))
            return _

        lax.fori_loop(low_p, high_p, step, None)

    @pl.when(gives)
    def _():
        planes(2, cz - 2, lambda copy: copy.start())
        for copy in last_phi:
            copy.start()

    for k in range(2):
        for a in range(3):
            g[a, k, 0:nx] = own[a, cz - 2 + k]

    @pl.when(odd)
    def _():
        pl.semaphore_wait(go, 1)

    loads[2].wait()
    loads[3].wait()
    loads[4].wait()

    @pl.when(gets_via)
    def _():
        for landed, onward in zip(via, far):
            landed.wait_recv()
            onward.start()

    def sideways(fields, planes, group):
        return (
            pltpu.make_async_remote_copy(
                src_ref=g.at[fields, planes, nx - ROWS : nx], dst_ref=from_left.at[fields, planes],
                send_sem=lat_send.at[0, group], recv_sem=lat_recv.at[0, group],
                device_id={"lat": right}, device_id_type=MESH),
            pltpu.make_async_remote_copy(
                src_ref=g.at[fields, planes, 0:ROWS], dst_ref=from_right.at[fields, planes],
                send_sem=lat_send.at[1, group], recv_sem=lat_recv.at[1, group],
                device_id={"lat": left}, device_id_type=MESH),
        )

    everything, phases, chemical = slice(0, 5), slice(0, 3), slice(3, 5)
    lat_own = sideways(everything, slice(1, 2), 0)
    lat_head_chem = sideways(chemical, slice(2, 4), 1)
    lat_end_chem = sideways(chemical, slice(top, top + 1), 2)
    lat_chem = sideways(chemical, slice(4, top), 3)

    lat_pair = sideways(phases, slice(cz, top), 4 + cz - 2)
    lat_head = sideways(phases, slice(2, 4), 4 + cz - 1)

    def lat_plane(p):
        return sideways(phases, pl.ds(p + 2, 1), 4 + p)

    def start(pair):
        for copy in pair:
            copy.start()

    def wait(pair):
        for copy in pair:
            copy.wait()

    def merge(fields, z):
        for f in fields:
            g[f, z, nx : nx + ROWS] = jnp.where(row < 4, from_right[f, z], from_left[f, z])

    def tile_step(src, z, t):
        def part(f, z, t):
            return src[f, z, t * ROWS : (t + 1) * ROWS]

        after, before = (t + 1) % (tiles + 1), (t + tiles) % (tiles + 1)
        centre, lap = [], []
        for f in range(5):
            c = part(f, z, t)
            up = pltpu.roll(jnp.where(row == 0, part(f, z, after), c), ROWS - 1, 0)
            down = pltpu.roll(jnp.where(row == ROWS - 1, part(f, z, before), c), 1, 0)
            lap.append(
                ((part(f, z + 1, t) + part(f, z - 1, t)) + (up + down))
                + (pltpu.roll(c, ny - 1, 1) + pltpu.roll(c, 1, 1)) - 6.0 * c)
            centre.append(c)
        plane = ((me + 1) * cz - 2 + z).astype(jnp.float32)
        temp = 2.0 * (plane + 0.5) / float(n * cz) - 1.0
        return advance(centre[:3], centre[3:], lap, temp)

    def first(z, parts):
        for t in parts:
            new, chem = tile_step(g, z, t)
            for f, value in enumerate(new[:3] + chem):
                half[f, z, t * ROWS : (t + 1) * ROWS] = value

    def second(z):
        for t in inner:
            new, chem = tile_step(half, z, t)
            for f, value in enumerate(new + chem):
                staged[f, z - 2, t * ROWS : (t + 1) * ROWS] = value

    def chem_in():
        start(lat_own)
        body_chem.wait_recv()
        start(lat_chem)
        wait(lat_own)
        merge(range(5), 1)
        wait(lat_chem)
        lax.fori_loop(4, top, lambda z, _: merge((3, 4), z), None)

    def head_chem_lands():
        wait(lat_head_chem)
        lax.fori_loop(2, 4, lambda z, _: merge((3, 4), z), None)

    @pl.when(jnp.logical_and(even, gets_end))
    def _():
        end[0].wait_recv()
        pass_chem.start()
        start(lat_end_chem)
        end[1].wait_recv()
        start(lat_plane(cz))
        end[2].wait_recv()
        for copy in pass_phi:
            copy.start()

    @pl.when(gets)
    def _():
        lead_chem.wait_recv()

    @pl.when(odd_end)
    def _():
        for copy in end:
            copy.start()

    @pl.when(gets)
    def _():
        chem_in()

    @pl.when(jnp.logical_and(gets, even))
    def _():
        head_chem.wait_recv()
        start(lat_head_chem)
        head_chem_lands()

    code = jnp.where(even, 0, jnp.where(corner == 1, 1, 2))
    plans = [schedule(kind, cz) for kind in range(3)]
    longest = max(len(plan) for plan in plans)
    words = []
    for k in range(longest):
        packed = [pack(plan[k]) if k < len(plan) else (0, 0) for plan in plans]
        words.append([jnp.where(code == 0, p0, jnp.where(code == 1, p1, p2)) for p0, p1, p2 in zip(*packed)])
    count = jnp.where(code == 0, len(plans[0]), jnp.where(code == 1, len(plans[1]), len(plans[2])))
    count = jnp.where(gets, count, 0)
    topmost = jnp.logical_not(gets_end)

    def run(k, _):
        comm, work = words[0]
        for q in range(1, longest):
            comm = jnp.where(k == q, words[q][0], comm)
            work = jnp.where(k == q, words[q][1], work)
        event, sent, landed = comm % BASE, comm // BASE % BASE, comm // (BASE * BASE)

        @pl.when(event == PLANE)
        def _():
            plane_phi(sent - 1).wait_recv()

        @pl.when(event == EDGES)
        def _():
            last_phi[0].wait_recv()
            last_phi[1].wait_recv()
            start(lat_pair)

        @pl.when(event == MID)
        def _():
            last_phi[2].wait_recv()

        @pl.when(event == LAST)
        def _():
            last_phi[3].wait_recv()

        @pl.when(event == HEAD)
        def _():
            head_chem.wait_recv()
            start(lat_head_chem)
            pass_phi[0].wait_recv()
            pass_phi[1].wait_recv()
            start(lat_head)

        @pl.when(event == PASS_MID)
        def _():
            pass_phi[2].wait_recv()

        @pl.when(event == PASS_LAST)
        def _():
            pass_phi[3].wait_recv()

        @pl.when(event == END)
        def _():
            end[0].wait_recv()
            start(lat_end_chem)
            end[1].wait_recv()

        @pl.when(event == END_NEXT)
        def _():
            end[2].wait_recv()

        @pl.when(jnp.logical_or(event == PLANE, event == END))
        def _():
            start(lat_plane(sent - 1))

        ending = landed == cz + 1

        @pl.when(jnp.logical_and(ending, gets_end))
        def _():
            wait(lat_end_chem)
            merge((3, 4), top)

        @pl.when(jnp.logical_or(jnp.logical_and(landed > 0, landed < cz - 1), jnp.logical_and(ending, gets_end)))
        def _():
            wait(lat_plane(landed - 1))
            merge(range(3), landed + 1)

        @pl.when(landed == cz - 1)
        def _():
            wait(lat_pair)
            lax.fori_loop(cz, top, lambda z, _: merge(range(3), z), None)

        @pl.when(landed == cz)
        def _():
            head_chem_lands()
            wait(lat_head)
            lax.fori_loop(2, 4, lambda z, _: merge(range(3), z), None)

        @pl.when(jnp.logical_and(topmost, landed == cz - 1))
        def _():
            for f in range(5):
                g[f, top, nx:] = g[f, top - 1, nx:]

        @pl.when(jnp.logical_and(topmost, event == LAST))
        def _():
            for f in range(5):
                g[f, top, 0:nx] = g[f, top - 1, 0:nx]

        def span(value):
            low_z = value % BASE
            return low_z, low_z + value // BASE

        h0, h1 = span(work % (4 * BASE))
        f0, f1 = span(work // (4 * BASE) % (4 * BASE))
        s0, s1 = span(work // (16 * BASE * BASE))
        lax.fori_loop(h0, h1, lambda z, _: first(z, (tiles,)), None)
        lax.fori_loop(f0, jnp.minimum(f1, jnp.where(topmost, top, top + 1)), lambda z, _: first(z, inner), None)

        @pl.when(jnp.logical_and(topmost, event == LAST))
        def _():
            for f in range(5):
                half[f, top, 0:nx] = half[f, top - 1, 0:nx]

        lax.fori_loop(s0, s1, lambda z, _: second(z), None)
        return _

    lax.fori_loop(0, count, run, None)

    @pl.when(jnp.logical_not(gets))
    def _():
        def entering(o, _):
            kind = index[o]
            for a in range(4):
                staged[a, o] = jnp.full((nx, ny), 1.0 if a == 0 else 0.0, jnp.float32)
            for k in range(2):
                value = jnp.zeros((nx, ny), jnp.float32)
                for liquid in range(table.shape[1]):
                    value = jnp.where(kind == liquid, table[k, liquid], value)
                staged[4 + k, o] = value
            return _

        lax.fori_loop(0, cz, entering, None)

    @pl.when(gives_end)
    def _():
        for copy in end:
            copy.wait_send()

    @pl.when(gives_via)
    def _():
        for copy in via:
            copy.wait_send()

    @pl.when(gets_via)
    def _():
        for copy in far:
            copy.wait_send()

    @pl.when(odd)
    def _():
        head_chem.wait_send()
        plane_phi(0).wait_send()
        plane_phi(1).wait_send()

    @pl.when(gives)
    def _():
        lead_chem.wait_send()
        body_chem.wait_send()
        planes(2, cz - 2, lambda copy: copy.wait_send())
        for copy in last_phi:
            copy.wait_send()

    @pl.when(jnp.logical_and(even, gets_end))
    def _():
        pass_chem.wait_send()
        for copy in pass_phi:
            copy.wait_send()


def flush(staged, phase_out, chem_out, sem):
    copies = (
        pltpu.make_async_copy(staged.at[0:4], phase_out, sem.at[0]),
        pltpu.make_async_copy(staged.at[4:6], chem_out, sem.at[1]),
    )
    for copy in copies:
        copy.start()
    for copy in copies:
        copy.wait()


def body(labels, seed_blend, potential, inflow_index, liquid_table):
    n, m = lax.axis_size("grow"), lax.axis_size("lat")
    cz, nx, ny = labels.shape
    dma = pltpu.SemaphoreType.DMA
    f32 = jnp.float32
    vmem, hbm = pl.BlockSpec(memory_space=pltpu.VMEM), pl.BlockSpec(memory_space=pltpu.HBM)
    staged = pl.pallas_call(
        functools.partial(kernel, n, m),
        out_shape=pltpu.VMEM((6, cz, nx, ny), f32),
        in_specs=[hbm] * 5,
        out_specs=vmem,
        scratch_shapes=[
            pltpu.SMEM(liquid_table.shape[::-1], f32),
            pltpu.VMEM((cz, nx, ny), jnp.int32),
            pltpu.VMEM((4, cz, nx, ny), f32),
            pltpu.VMEM((cz, nx, ny), jnp.int32),
            pltpu.VMEM((3, cz, nx, ny), f32),
            pltpu.VMEM((5, cz + 4, nx + ROWS, ny), f32),
            pltpu.VMEM((5, cz + 4, nx + ROWS, ny), f32),
            pltpu.VMEM((5, cz + 4, ROWS, ny), f32),
            pltpu.VMEM((5, cz + 4, ROWS, ny), f32),
            pltpu.VMEM((5, 2, nx, ny), f32),
            dma((5,)),
            dma((18,)),
            dma((17,)),
            dma((cz,)),
            dma((cz,)),
            dma((2, 5 + cz)),
            dma((2, 5 + cz)),
            pltpu.SemaphoreType.REGULAR,
        ],
        compiler_params=pltpu.CompilerParams(collective_id=0, has_side_effects=True, vmem_limit_bytes=12 << 20),
    )(*(pltpu.with_memory_space_constraint(a, pltpu.HBM) for a in (labels, seed_blend, potential, inflow_index, liquid_table.T)))
    return pl.pallas_call(
        flush,
        out_shape=(jax.ShapeDtypeStruct((4, cz, nx, ny), f32), jax.ShapeDtypeStruct((2, cz, nx, ny), f32)),
        in_specs=[pl.BlockSpec(memory_space=pl.ANY)],
        out_specs=(hbm, hbm),
        scratch_shapes=[dma((2,))],
        compiler_params=pltpu.CompilerParams(vmem_limit_bytes=1 << 20),
    )(pltpu.with_memory_space_constraint(staged, pltpu.VMEM))


def solution(mesh):
    in_specs = (
        P("grow", "lat", None),
        P(None, "grow", "lat", None),
        P(None, "grow", "lat", None),
        P(None, "lat", None),
        P(),
    )
    out_specs = (P(None, "grow", "lat", None), P(None, "grow", "lat", None))
    return jax.shard_map(body, mesh=mesh, in_specs=in_specs, out_specs=out_specs, check_vma=False)
```

time: 40.6 us -> 39.2 us (0.966)
  Pallas kernels: 39.8 us -> 38.2 us
    pallas_call x1, Pallas kernels: 38.7 us -> 37.1 us  [body(): pl.pallas_call(functools.partial(kernel, n, m), out_shape=pltpu.VMEM((6,...]
where the time goes in v3:
time: 39.2 us; the launch traced here: 38.9 us
  Pallas kernels  38.2 us (97%)
  between operations  0.64 us (2%)
    pallas_call x1, Pallas kernels, body(): pl.pallas_call(functools.partial(kernel, n, m), out_shape=pltpu.VMEM((6,...  37.1 us
    pallas_call x1, Pallas kernels, body(): pl.pallas_call(flush, out_shape=(jax.ShapeDtypeStruct((4, cz, nx, ny), f3...  1.16 us

profile of v3, /device:TPU:7, one launch (start us, length us, event | category | flops | bytes accessed | tf_op | source)
XLA Modules:
  0.0 38.9 jit_solution(3054738342013094509)
XLA Ops:
  0.6 37.1 %shard_map.68.staged = f32[6,8,32,256]{3,2,1,0:T(8,128)S(1)} custom-call(s32[8,32,256]{2,1,0:T(8,128)} %labels_h.1, f32[4,8,32,256]{3,2,1,0:T(8,128)} %blend_h.1, f32[2,8,32,256]{3,2,1,0:T(8,128)} %chem_h.1, s32[8,32,256]{2,1,0:T(8,128)} %index_h.1, f32[2,16]{1,0:T(2,128)} %bitcast.1), custom_call_target="tpu_custom_call" | custom-call | tf_op jit(solution)/shard_map/pallas_call | solution.py:589
  37.7 1.2 %shard_map.69 = (f32[4,8,32,256]{3,2,1,0:T(8,128)}, f32[2,8,32,256]{3,2,1,0:T(8,128)}) custom-call(f32[6,8,32,256]{3,2,1,0:T(8,128)S(1)} %shard_map.68.staged), custom_call_target="tpu_custom_call" | custom-call | tf_op jit(solution)/shard_map/pallas_call | solution.py:616

commit v4 on v3

--- a/solution.py
+++ b/solution.py
@@ -13,6 +13,7 @@
 diffusion = 0.05
 MESH = pl.DeviceIdType.MESH
 ROWS = 8
+LATE = 3
 
 
 def advance(phi, chem, lap, temp):
@@ -43,7 +44,27 @@
     return new, out
 
 
-BASE = 32
+def tile_step(src, z, t, tiles, plane, planes):
+    ny = src.shape[-1]
+    row = lax.broadcasted_iota(jnp.int32, (ROWS, ny), 0)
+
+    def part(f, z, t):
+        return src[f, z, t * ROWS : (t + 1) * ROWS]
+
+    after, before = (t + 1) % (tiles + 1), (t + tiles) % (tiles + 1)
+    centre, lap = [], []
+    for f in range(5):
+        c = part(f, z, t)
+        up = pltpu.roll(jnp.where(row == 0, part(f, z, after), c), ROWS - 1, 0)
+        down = pltpu.roll(jnp.where(row == ROWS - 1, part(f, z, before), c), 1, 0)
+        lap.append(
+            ((part(f, z + 1, t) + part(f, z - 1, t)) + (up + down))
+            + (pltpu.roll(c, ny - 1, 1) + pltpu.roll(c, 1, 1)) - 6.0 * c)
+        centre.append(c)
+    temp = 2.0 * (plane.astype(jnp.float32) + 0.5) / float(planes) - 1.0
+    return advance(centre[:3], centre[3:], lap, temp)
+
+
 PLANE, EDGES, MID, LAST, HEAD, PASS_MID, PASS_LAST, END, END_NEXT = range(1, 10)
 
 
@@ -92,12 +113,15 @@
         step(PLANE, 5),
         *(step(PLANE, p, p - 1, (p, 1), (p, 1), (p - 1, 1) if p > 6 else none) for p in range(6, pair)),
         step(HEAD, head, pair - 1, (pair, 1), (pair, 1), (pair - 1, 1) if pair > 6 else none),
-        step(EDGES, pair, head, (2, 3)),
-        step(PASS_MID, None, None, none, (4, 1), (5, 1)),
+        step(PASS_MID, None, head, (2, 3), (4, 1), (5, 1)),
+        step(EDGES, pair),
         step(PASS_LAST, None, None, none, (1, 3), (2, 3)),
         step(MID, None, pair, (pair + 1, 3), (pair + 1, 1), (pair, 1)),
         step(LAST, None, None, none, (cz, 3), (cz - 1, 3)),
     ]
+
+
+BASE = 32
 
 
 def pack(step):
@@ -108,8 +132,18 @@
     return event + BASE * (sent + BASE * landed), work
 
 
-def kernel(n, m, labels_h, blend_h, chem_h, index_h, table_h, staged,
-           table, labels, blend, index, own, g, half, from_right, from_left, relay,
+def pick(k, values):
+    bit = 1
+    while len(values) > 1:
+        odd = k // bit % 2 == 1
+        paired = [jnp.where(odd, b, a) for a, b in zip(values[0::2], values[1::2])]
+        values = paired + values[len(values) - len(values) % 2 :]
+        bit *= 2
+    return values[0]
+
+
+def kernel(n, m, labels_h, blend_h, chem_h, index_h, table_h, staged, half,
+           table, labels, blend, index, own, g, from_right, from_left, relay,
            load_sem, send_sem, recv_sem, plane_send, plane_recv, lat_send, lat_recv, go):
     cz, nx, ny = labels.shape
     tiles = nx // ROWS
@@ -326,33 +360,15 @@
         for f in fields:
             g[f, z, nx : nx + ROWS] = jnp.where(row < 4, from_right[f, z], from_left[f, z])
 
-    def tile_step(src, z, t):
-        def part(f, z, t):
-            return src[f, z, t * ROWS : (t + 1) * ROWS]
-
-        after, before = (t + 1) % (tiles + 1), (t + tiles) % (tiles + 1)
-        centre, lap = [], []
-        for f in range(5):
-            c = part(f, z, t)
-            up = pltpu.roll(jnp.where(row == 0, part(f, z, after), c), ROWS - 1, 0)
-            down = pltpu.roll(jnp.where(row == ROWS - 1, part(f, z, before), c), 1, 0)
-            lap.append(
-                ((part(f, z + 1, t) + part(f, z - 1, t)) + (up + down))
-                + (pltpu.roll(c, ny - 1, 1) + pltpu.roll(c, 1, 1)) - 6.0 * c)
-            centre.append(c)
-        plane = ((me + 1) * cz - 2 + z).astype(jnp.float32)
-        temp = 2.0 * (plane + 0.5) / float(n * cz) - 1.0
-        return advance(centre[:3], centre[3:], lap, temp)
-
     def first(z, parts):
         for t in parts:
-            new, chem = tile_step(g, z, t)
+            new, chem = tile_step(g, z, t, tiles, (me + 1) * cz - 2 + z, n * cz)
             for f, value in enumerate(new[:3] + chem):
                 half[f, z, t * ROWS : (t + 1) * ROWS] = value
 
     def second(z):
         for t in inner:
-            new, chem = tile_step(half, z, t)
+            new, chem = tile_step(half, z, t, tiles, (me + 1) * cz - 2 + z, n * cz)
             for f, value in enumerate(new + chem):
                 staged[f, z - 2, t * ROWS : (t + 1) * ROWS] = value
 
@@ -401,9 +417,8 @@
 
     code = jnp.where(even, 0, jnp.where(corner == 1, 1, 2))
     plans = [schedule(kind, cz) for kind in range(3)]
-    longest = max(len(plan) for plan in plans)
     words = []
-    for k in range(longest):
+    for k in range(max(len(plan) for plan in plans)):
         packed = [pack(plan[k]) if k < len(plan) else (0, 0) for plan in plans]
         words.append([jnp.where(code == 0, p0, jnp.where(code == 1, p1, p2)) for p0, p1, p2 in zip(*packed)])
     count = jnp.where(code == 0, len(plans[0]), jnp.where(code == 1, len(plans[1]), len(plans[2])))
@@ -411,11 +426,16 @@
     topmost = jnp.logical_not(gets_end)
 
     def run(k, _):
-        comm, work = words[0]
-        for q in range(1, longest):
-            comm = jnp.where(k == q, words[q][0], comm)
-            work = jnp.where(k == q, words[q][1], work)
+        comm, work = pick(k, [w[0] for w in words]), pick(k, [w[1] for w in words])
         event, sent, landed = comm % BASE, comm // BASE % BASE, comm // (BASE * BASE)
+
+        def span(value):
+            low_z = value % BASE
+            return low_z, low_z + value // BASE
+
+        h0, h1 = span(work % (4 * BASE))
+        f0, f1 = span(work // (4 * BASE) % (4 * BASE))
+        s0, s1 = span(work // (16 * BASE * BASE))
 
         @pl.when(event == PLANE)
         def _():
@@ -498,13 +518,6 @@
             for f in range(5):
                 g[f, top, 0:nx] = g[f, top - 1, 0:nx]
 
-        def span(value):
-            low_z = value % BASE
-            return low_z, low_z + value // BASE
-
-        h0, h1 = span(work % (4 * BASE))
-        f0, f1 = span(work // (4 * BASE) % (4 * BASE))
-        s0, s1 = span(work // (16 * BASE * BASE))
         lax.fori_loop(h0, h1, lambda z, _: first(z, (tiles,)), None)
         lax.fori_loop(f0, jnp.minimum(f1, jnp.where(topmost, top, top + 1)), lambda z, _: first(z, inner), None)
 
@@ -513,7 +526,7 @@
             for f in range(5):
                 half[f, top, 0:nx] = half[f, top - 1, 0:nx]
 
-        lax.fori_loop(s0, s1, lambda z, _: second(z), None)
+        lax.fori_loop(s0, jnp.minimum(s1, cz + 2 - LATE), lambda z, _: second(z), None)
         return _
 
     lax.fori_loop(0, count, run, None)
@@ -569,15 +582,53 @@
             copy.wait_send()
 
 
-def flush(staged, phase_out, chem_out, sem):
-    copies = (
-        pltpu.make_async_copy(staged.at[0:4], phase_out, sem.at[0]),
-        pltpu.make_async_copy(staged.at[4:6], chem_out, sem.at[1]),
-    )
-    for copy in copies:
+def flush(n, staged, half, phase_out, chem_out, final, sem):
+    cz, nx = staged.shape[1:3]
+    early, tiles = cz - LATE, nx // ROWS
+    me = lax.axis_index("grow")
+
+    def out(src, low, count, k):
+        return (
+            pltpu.make_async_copy(src.at[0:4], phase_out.at[:, pl.ds(low, count)], sem.at[0, k]),
+            pltpu.make_async_copy(src.at[4:6], chem_out.at[:, pl.ds(low, count)], sem.at[1, k]),
+        )
+
+    first_part = out(staged.at[:, 0:early], 0, early, LATE)
+    for copy in first_part:
         copy.start()
-    for copy in copies:
+
+    def late(q):
+        return out(final.at[:, pl.ds(q, 1)], early + q, 1, q)
+
+    def plane(q, _):
+        z = q + early + 2
+
+        @pl.when(me < n - 1)
+        def _():
+            for t in range(tiles):
+                new, chem = tile_step(half, z, t, tiles, (me + 1) * cz - 2 + z, n * cz)
+                for f, value in enumerate(new + chem):
+                    final[f, q, t * ROWS : (t + 1) * ROWS] = value
+
+        @pl.when(me == n - 1)
+        def _():
+            for f in range(6):
+                final[f, q] = staged[f, early + q]
+
+        for copy in late(q):
+            copy.start()
+        return _
+
+    lax.fori_loop(0, LATE, plane, None)
+    for copy in first_part:
         copy.wait()
+
+    def written(q, _):
+        for copy in late(q):
+            copy.wait()
+        return _
+
+    lax.fori_loop(0, LATE, written, None)
 
 
 def body(labels, seed_blend, potential, inflow_index, liquid_table):
@@ -586,18 +637,17 @@
     dma = pltpu.SemaphoreType.DMA
     f32 = jnp.float32
     vmem, hbm = pl.BlockSpec(memory_space=pltpu.VMEM), pl.BlockSpec(memory_space=pltpu.HBM)
-    staged = pl.pallas_call(
+    state = pl.pallas_call(
         functools.partial(kernel, n, m),
-        out_shape=pltpu.VMEM((6, cz, nx, ny), f32),
+        out_shape=(pltpu.VMEM((6, cz, nx, ny), f32), pltpu.VMEM((5, cz + 4, nx + ROWS, ny), f32)),
         in_specs=[hbm] * 5,
-        out_specs=vmem,
+        out_specs=(vmem, vmem),
         scratch_shapes=[
             pltpu.SMEM(liquid_table.shape[::-1], f32),
             pltpu.VMEM((cz, nx, ny), jnp.int32),
             pltpu.VMEM((4, cz, nx, ny), f32),
             pltpu.VMEM((cz, nx, ny), jnp.int32),
             pltpu.VMEM((3, cz, nx, ny), f32),
-            pltpu.VMEM((5, cz + 4, nx + ROWS, ny), f32),
             pltpu.VMEM((5, cz + 4, nx + ROWS, ny), f32),
             pltpu.VMEM((5, cz + 4, ROWS, ny), f32),
             pltpu.VMEM((5, cz + 4, ROWS, ny), f32),
@@ -614,13 +664,13 @@
         compiler_params=pltpu.CompilerParams(collective_id=0, has_side_effects=True, vmem_limit_bytes=12 << 20),
     )(*(pltpu.with_memory_space_constraint(a, pltpu.HBM) for a in (labels, seed_blend, potential, inflow_index, liquid_table.T)))
     return pl.pallas_call(
-        flush,
+        functools.partial(flush, n),
         out_shape=(jax.ShapeDtypeStruct((4, cz, nx, ny), f32), jax.ShapeDtypeStruct((2, cz, nx, ny), f32)),
-        in_specs=[pl.BlockSpec(memory_space=pl.ANY)],
+        in_specs=[vmem, vmem],
         out_specs=(hbm, hbm),
-        scratch_shapes=[dma((2,))],
-        compiler_params=pltpu.CompilerParams(vmem_limit_bytes=1 << 20),
-    )(pltpu.with_memory_space_constraint(staged, pltpu.VMEM))
+        scratch_shapes=[pltpu.VMEM((6, LATE, nx, ny), f32), dma((2, LATE + 1))],
+        compiler_params=pltpu.CompilerParams(vmem_limit_bytes=4 << 20),
+    )(*(pltpu.with_memory_space_constraint(a, pltpu.VMEM) for a in state))
 
 
 def solution(mesh):

time: 39.2 us -> 38.7 us (0.987)
  no operation moved by 1% of the time
where the time goes in v4:
time: 38.7 us; the launch traced here: 38.5 us
  Pallas kernels  37.9 us (98%)
  between operations  0.64 us (2%)
    pallas_call x1, Pallas kernels, body(): pl.pallas_call(functools.partial(kernel, n, m), out_shape=(pltpu.VMEM((6,...  36.5 us
    pallas_call x1, Pallas kernels, body(): pl.pallas_call(functools.partial(flush, n), out_shape=(jax.ShapeDtypeStru...  1.38 us

profile of v4, /device:TPU:7, one launch (start us, length us, event | category | flops | bytes accessed | tf_op | source)
XLA Modules:
  0.0 38.5 jit_solution(12736091935920809999)
XLA Ops:
  0.6 36.5 %shard_map.68 = (f32[6,8,32,256]{3,2,1,0:T(8,128)S(1)}, f32[5,12,40,256]{3,2,1,0:T(8,128)S(1)}) custom-call(s32[8,32,256]{2,1,0:T(8,128)} %labels_h.1, f32[4,8,32,256]{3,2,1,0:T(8,128)} %blend_h.1, f32[2,8,32,256]{3,2,1,0:T(8,128)} %chem_h.1, s32[8,32,256]{2,1,0:T(8,128)} %index_h.1, f32[2,16]{1,0:T(2,128)} %bitcast.1), custom_call_target="tpu_custom_call" | custom-call | tf_op jit(solution)/shard_map/pallas_call | solution.py:640
  37.2 1.4 %shard_map.69 = (f32[4,8,32,256]{3,2,1,0:T(8,128)}, f32[2,8,32,256]{3,2,1,0:T(8,128)}) custom-call(f32[6,8,32,256]{3,2,1,0:T(8,128)S(1)} %get-tuple-element.4.staged, f32[5,12,40,256]{3,2,1,0:T(8,128)S(1)} %get-tuple-element.5.half), custom_call_target="tpu_custom_call" | custom-call | tf_op jit(solution)/shard_map/pallas_call | solution.py:666

commit v5 on v4

--- a/solution.py
+++ b/solution.py
@@ -65,7 +65,7 @@
     return advance(centre[:3], centre[3:], lap, temp)
 
 
-PLANE, EDGES, MID, LAST, HEAD, PASS_MID, PASS_LAST, END, END_NEXT = range(1, 10)
+PLANE, EDGES, MID, LAST, HEAD, PASS_MID, PASS_LAST, END, END_NEXT, BOTH = range(1, 11)
 
 
 def schedule(kind, cz):
@@ -116,8 +116,7 @@
         step(PASS_MID, None, head, (2, 3), (4, 1), (5, 1)),
         step(EDGES, pair),
         step(PASS_LAST, None, None, none, (1, 3), (2, 3)),
-        step(MID, None, pair, (pair + 1, 3), (pair + 1, 1), (pair, 1)),
-        step(LAST, None, None, none, (cz, 3), (cz - 1, 3)),
+        step(BOTH, None, pair, (pair + 1, 3), (pair + 1, 4), (pair, 4)),
     ]
 
 
@@ -128,7 +127,7 @@
     event, sent, landed, halo, own, two = step
     work = 0
     for low, number in (two, own, halo):
-        work = work * (4 * BASE) + low + BASE * number
+        work = work * (8 * BASE) + low + BASE * number
     return event + BASE * (sent + BASE * landed), work
 
 
@@ -433,9 +432,9 @@
             low_z = value % BASE
             return low_z, low_z + value // BASE
 
-        h0, h1 = span(work % (4 * BASE))
-        f0, f1 = span(work // (4 * BASE) % (4 * BASE))
-        s0, s1 = span(work // (16 * BASE * BASE))
+        h0, h1 = span(work % (8 * BASE))
+        f0, f1 = span(work // (8 * BASE) % (8 * BASE))
+        s0, s1 = span(work // (64 * BASE * BASE))
 
         @pl.when(event == PLANE)
         def _():
@@ -447,11 +446,11 @@
             last_phi[1].wait_recv()
             start(lat_pair)
 
-        @pl.when(event == MID)
+        @pl.when(jnp.logical_or(event == MID, event == BOTH))
         def _():
             last_phi[2].wait_recv()
 
-        @pl.when(event == LAST)
+        @pl.when(jnp.logical_or(event == LAST, event == BOTH))
         def _():
             last_phi[3].wait_recv()
 
@@ -518,7 +517,13 @@
             for f in range(5):
                 g[f, top, 0:nx] = g[f, top - 1, 0:nx]
 
-        lax.fori_loop(h0, h1, lambda z, _: first(z, (tiles,)), None)
+        def halo_pair(q, _):
+            for step in range(2):
+                first(h0 + 2 * q + step, (tiles,))
+            return _
+
+        lax.fori_loop(0, (h1 - h0) // 2, halo_pair, None)
+        lax.fori_loop(h1 - (h1 - h0) % 2, h1, lambda z, _: first(z, (tiles,)), None)
         lax.fori_loop(f0, jnp.minimum(f1, jnp.where(topmost, top, top + 1)), lambda z, _: first(z, inner), None)
 
         @pl.when(jnp.logical_and(topmost, event == LAST))

time: 38.7 us -> 38.4 us (level)
  no operation moved by 1% of the time
where the time goes in v5:
time: 38.4 us; the launch traced here: 38.2 us
  Pallas kernels  37.6 us (98%)
  between operations  0.64 us (2%)
    pallas_call x1, Pallas kernels, body(): pl.pallas_call(functools.partial(kernel, n, m), out_shape=(pltpu.VMEM((6,...  36.2 us
    pallas_call x1, Pallas kernels, body(): pl.pallas_call(functools.partial(flush, n), out_shape=(jax.ShapeDtypeStru...  1.38 us

profile of v5, /device:TPU:7, one launch (start us, length us, event | category | flops | bytes accessed | tf_op | source)
XLA Modules:
  0.0 38.2 jit_solution(17485811866008101288)
XLA Ops:
  0.6 36.2 %shard_map.68 = (f32[6,8,32,256]{3,2,1,0:T(8,128)S(1)}, f32[5,12,40,256]{3,2,1,0:T(8,128)S(1)}) custom-call(s32[8,32,256]{2,1,0:T(8,128)} %labels_h.1, f32[4,8,32,256]{3,2,1,0:T(8,128)} %blend_h.1, f32[2,8,32,256]{3,2,1,0:T(8,128)} %chem_h.1, s32[8,32,256]{2,1,0:T(8,128)} %index_h.1, f32[2,16]{1,0:T(2,128)} %bitcast.1), custom_call_target="tpu_custom_call" | custom-call | tf_op jit(solution)/shard_map/pallas_call | solution.py:645
  36.8 1.4 %shard_map.69 = (f32[4,8,32,256]{3,2,1,0:T(8,128)}, f32[2,8,32,256]{3,2,1,0:T(8,128)}) custom-call(f32[6,8,32,256]{3,2,1,0:T(8,128)S(1)} %get-tuple-element.4.staged, f32[5,12,40,256]{3,2,1,0:T(8,128)S(1)} %get-tuple-element.5.half), custom_call_target="tpu_custom_call" | custom-call | tf_op jit(solution)/shard_map/pallas_call | solution.py:671

commit v6 on v5

--- a/solution.py
+++ b/solution.py
@@ -65,7 +65,7 @@
     return advance(centre[:3], centre[3:], lap, temp)
 
 
-PLANE, EDGES, MID, LAST, HEAD, PASS_MID, PASS_LAST, END, END_NEXT, BOTH = range(1, 11)
+PLANE, EDGES, MID, LAST, HEAD, PASS_MID, PASS_LAST, END, END_NEXT, BOTH, CROSS = range(1, 12)
 
 
 def schedule(kind, cz):
@@ -114,8 +114,7 @@
         *(step(PLANE, p, p - 1, (p, 1), (p, 1), (p - 1, 1) if p > 6 else none) for p in range(6, pair)),
         step(HEAD, head, pair - 1, (pair, 1), (pair, 1), (pair - 1, 1) if pair > 6 else none),
         step(PASS_MID, None, head, (2, 3), (4, 1), (5, 1)),
-        step(EDGES, pair),
-        step(PASS_LAST, None, None, none, (1, 3), (2, 3)),
+        step(CROSS, pair, None, none, (1, 3), (2, 3)),
         step(BOTH, None, pair, (pair + 1, 3), (pair + 1, 4), (pair, 4)),
     ]
 
@@ -440,7 +439,7 @@
         def _():
             plane_phi(sent - 1).wait_recv()
 
-        @pl.when(event == EDGES)
+        @pl.when(jnp.logical_or(event == EDGES, event == CROSS))
         def _():
             last_phi[0].wait_recv()
             last_phi[1].wait_recv()
@@ -466,7 +465,7 @@
         def _():
             pass_phi[2].wait_recv()
 
-        @pl.when(event == PASS_LAST)
+        @pl.when(jnp.logical_or(event == PASS_LAST, event == CROSS))
         def _():
             pass_phi[3].wait_recv()
 

time: 38.4 us -> 38.2 us (level)
  no operation moved by 1% of the time
where the time goes in v6:
time: 38.2 us; the launch traced here: 38 us
  Pallas kernels  37.4 us (98%)
  between operations  0.64 us (2%)
    pallas_call x1, Pallas kernels, body(): pl.pallas_call(functools.partial(kernel, n, m), out_shape=(pltpu.VMEM((6,...  36 us
    pallas_call x1, Pallas kernels, body(): pl.pallas_call(functools.partial(flush, n), out_shape=(jax.ShapeDtypeStru...  1.38 us

profile of v6, /device:TPU:7, one launch (start us, length us, event | category | flops | bytes accessed | tf_op | source)
XLA Modules:
  0.0 38.0 jit_solution(6551827766619914424)
XLA Ops:
  0.6 36.0 %shard_map.68 = (f32[6,8,32,256]{3,2,1,0:T(8,128)S(1)}, f32[5,12,40,256]{3,2,1,0:T(8,128)S(1)}) custom-call(s32[8,32,256]{2,1,0:T(8,128)} %labels_h.1, f32[4,8,32,256]{3,2,1,0:T(8,128)} %blend_h.1, f32[2,8,32,256]{3,2,1,0:T(8,128)} %chem_h.1, s32[8,32,256]{2,1,0:T(8,128)} %index_h.1, f32[2,16]{1,0:T(2,128)} %bitcast.1), custom_call_target="tpu_custom_call" | custom-call | tf_op jit(solution)/shard_map/pallas_call | solution.py:644
  36.6 1.4 %shard_map.69 = (f32[4,8,32,256]{3,2,1,0:T(8,128)}, f32[2,8,32,256]{3,2,1,0:T(8,128)}) custom-call(f32[6,8,32,256]{3,2,1,0:T(8,128)S(1)} %get-tuple-element.4.staged, f32[5,12,40,256]{3,2,1,0:T(8,128)S(1)} %get-tuple-element.5.half), custom_call_target="tpu_custom_call" | custom-call | tf_op jit(solution)/shard_map/pallas_call | solution.py:670
